TPU v7x, 32 devices: a whole 2x2x4 slice. The times are simulated.
32 devices in a mesh: fsdp: 2 (over y), ctx: 4 (over x, core), tp: 4 (over z).
Axes of the slice: x: 2, y: 2, z: 4, core: 2. Of those that a mesh axis runs over, the one named last changes fastest.
Arguments:
- block_input: bfloat16 [4, 2048, 1024], P('fsdp', 'ctx'), may hold values from -6 to 6
- positions: int32 [3, 4, 2048], P(None, 'fsdp', 'ctx'), may hold values from 0 to 15
- w_qkv: bfloat16 [3, 1024, 1024], P(None, 'fsdp', 'tp'), may hold values from -0.1875 to 0.1875
- b_qkv: float32 [3, 1024], P(None, 'tp'), may hold values from -3 to 3
- w_proj: bfloat16 [1024, 1024], P('tp', 'fsdp'), may hold values from -1 to 1
- w_up: bfloat16 [1024, 4096], P('fsdp', 'tp'), may hold values from -0.1875 to 0.1875
- b_up: float32 [4096], P('tp'), may hold values from -3 to 3
- w_down: bfloat16 [4096, 1024], P('tp', 'fsdp'), may hold values from -0.09375 to 0.09375
- norm_gains: float32 [2, 1024], replicated, may hold values from 0.5 to 1.5
- norm_shifts: float32 [2, 1024], replicated, may hold values from -2 to 2
- out_shifts: float32 [2, 1024], replicated, may hold values from -2 to 2
- grad_out: bfloat16 [4, 2048, 1024], P('fsdp', 'ctx'), may hold values from -6 to 6
Outputs:
- block_output: bfloat16 [4, 2048, 1024], P('fsdp', 'ctx')
- grad_input: float32 [4, 2048, 1024], P('fsdp', 'ctx')
- grad_w_qkv: float32 [3, 1024, 1024], P(None, 'fsdp', 'tp')
- grad_b_qkv: float32 [3, 1024], P(None, 'tp')
- grad_w_proj: float32 [1024, 1024], P('tp', 'fsdp')
- grad_w_up: float32 [1024, 4096], P('fsdp', 'tp')
- grad_b_up: float32 [4096], P('tp')
- grad_w_down: float32 [4096, 1024], P('tp', 'fsdp')
- grad_gains: float32 [2, 1024], replicated
- grad_shifts: float32 [2, 1024], replicated
- grad_out_shifts: float32 [2, 1024], replicated
Inputs may be any that keep to these rules, and one draw needn't show every extreme that they name: `positions`: each token's time, height and width index in its clip.
All inputs are finite; a program needn't handle non-finite values.
Results may differ from a plain program's by a relative error of at most 0.02.
Values may be sent and summed in bfloat16 or wider, within the bound.
A program may use at most 128 MiB of HBM per device.

v0:
```python
from functools import partial
import jax
import jax.numpy as jnp
from jax import lax
from jax.sharding import PartitionSpec as P

HD = 64
LEN = 2048
ROT = 20
QBLK = 512
EPSILON = 1e-06


def layer_norm(values, gain_vec, shift_vec):
    center = values - jnp.mean(values, axis=-1, keepdims=True)
    spread = jnp.mean(center * center, axis=-1, keepdims=True)
    return center * lax.rsqrt(spread + EPSILON) * gain_vec + shift_vec


def rotary_tables(position_rows):
    half_rot = ROT // 2
    freqs = 10000.0 ** (-2.0 * jnp.arange(half_rot, dtype=jnp.float32) / ROT)
    angles = position_rows.astype(jnp.float32)[:, :, None] * freqs[None, None, :]
    return (jnp.cos(angles), jnp.sin(angles))


def rotary(values, cos_table, sin_table):
    half_rot = ROT // 2
    pieces = []
    for dim_index in range(3):
        offset_at = dim_index * ROT
        first_half = values[..., offset_at : offset_at + half_rot]
        second_half = values[..., offset_at + half_rot : offset_at + ROT]
        cos_part = cos_table[dim_index][:, None, :]
        sin_part = sin_table[dim_index][:, None, :]
        pieces.append(first_half * cos_part - second_half * sin_part)
        pieces.append(second_half * cos_part + first_half * sin_part)
    pieces.append(values[..., 3 * ROT :])
    return jnp.concatenate(pieces, axis=-1)


def contract_rows(left_mat, right_mat):
    return lax.dot_general(
        left_mat, right_mat, (((0,), (0,)), ((), ())), preferred_element_type=jnp.float32
    )


def contract_cols(left_mat, right_mat):
    return lax.dot_general(
        left_mat, right_mat, (((1,), (1,)), ((), ())), preferred_element_type=jnp.float32
    )


def tp_whole(partial_sum):
    return lax.psum(partial_sum.astype(jnp.bfloat16), "tp").astype(jnp.float32)


def attend_group(operands):
    queries, keys_all, values_all = operands
    score_factor = HD ** (-0.5)

    def attend_block(query_block):
        scores = (
            jnp.einsum("qe,ke->qk", query_block, keys_all, preferred_element_type=jnp.float32)
            * score_factor
        )
        largest = jnp.max(scores, axis=-1, keepdims=True)
        expon = jnp.exp(scores - largest)
        totals = jnp.sum(expon, axis=-1, keepdims=True)
        probs = expon / totals
        block_out = jnp.dot(
            probs.astype(jnp.bfloat16), values_all, preferred_element_type=jnp.float32
        )
        return (block_out.astype(jnp.bfloat16), (largest + jnp.log(totals))[:, 0])

    return lax.map(attend_block, queries.reshape(LEN // QBLK, QBLK, HD))


def backward_group(operands):
    queries, keys_all, values_all, grad_attended, log_totals = operands
    score_factor = HD ** (-0.5)

    def back_block(carry, block_items):
        grad_keys, grad_values = carry
        query_block, grad_block, log_block = block_items
        scores = (
            jnp.einsum("qe,ke->qk", query_block, keys_all, preferred_element_type=jnp.float32)
            * score_factor
        )
        probs = jnp.exp(scores - log_block[:, None])
        probs_low = probs.astype(jnp.bfloat16)
        grad_probs = jnp.einsum(
            "qe,ke->qk", grad_block, values_all, preferred_element_type=jnp.float32
        )
        inner = jnp.sum(probs * grad_probs, axis=-1, keepdims=True)
        grad_scores = (probs * (grad_probs - inner)).astype(jnp.bfloat16)
        grad_query = (
            jnp.dot(grad_scores, keys_all, preferred_element_type=jnp.float32) * score_factor
        )
        grad_keys = grad_keys + contract_rows(grad_scores, query_block) * score_factor
        grad_values = grad_values + contract_rows(probs_low, grad_block)
        return ((grad_keys, grad_values), grad_query)

    zeros_kv = jnp.zeros((LEN, HD), jnp.float32)
    block_count = LEN // QBLK
    items = (
        queries.reshape(block_count, QBLK, HD),
        grad_attended.reshape(block_count, QBLK, HD),
        log_totals,
    )
    (grad_keys, grad_values), grad_queries = lax.scan(back_block, (zeros_kv, zeros_kv), items)
    return (grad_queries.reshape(LEN, HD), grad_keys, grad_values)


def shards(
    block_input,
    positions,
    w_qkv,
    b_qkv,
    w_proj,
    w_up,
    b_up,
    w_down,
    norm_gains,
    norm_shifts,
    out_shifts,
    grad_out,
):
    clip_count, local_len, width = block_input.shape
    row_count = clip_count * local_len
    ctx_count = lax.axis_size("ctx")
    local_width = w_qkv.shape[2]
    group_heads = local_width // ctx_count // HD
    group_count = clip_count * group_heads
    inputs = block_input.reshape(row_count, width).astype(jnp.float32)
    full_qkv, full_proj, full_up, full_down = (
        lax.all_gather(w_qkv, "fsdp", axis=1, tiled=True),
        lax.all_gather(w_proj, "fsdp", axis=1, tiled=True),
        lax.all_gather(w_up, "fsdp", axis=0, tiled=True),
        lax.all_gather(w_down, "fsdp", axis=1, tiled=True),
    )
    cos_table, sin_table = rotary_tables(positions.reshape(3, row_count))
    normed_one = layer_norm(inputs, norm_gains[0], norm_shifts[0])
    normed_one_low = normed_one.astype(jnp.bfloat16)
    projected = (
        jnp.einsum("rd,cde->cre", normed_one_low, full_qkv, preferred_element_type=jnp.float32)
        + b_qkv[:, None, :]
    )
    head_shape = (row_count, local_width // HD, HD)
    queries_rot = rotary(projected[0].reshape(head_shape), cos_table, sin_table).reshape(
        row_count, local_width
    )
    keys_rot = rotary(projected[1].reshape(head_shape), cos_table, sin_table).reshape(
        row_count, local_width
    )
    token_qkv = (
        jnp.stack([queries_rot, keys_rot, projected[2]])
        .astype(jnp.bfloat16)
        .reshape(3, clip_count, local_len, local_width)
    )
    head_qkv = lax.all_to_all(token_qkv, "ctx", split_axis=3, concat_axis=2, tiled=True)
    full_len = head_qkv.shape[2]
    grouped = (
        head_qkv.reshape(3, clip_count, full_len, group_heads, HD)
        .transpose(0, 1, 3, 2, 4)
        .reshape(3, group_count, full_len, HD)
    )
    attended, log_totals = lax.map(attend_group, (grouped[0], grouped[1], grouped[2]))
    attended = (
        attended.reshape(clip_count, group_heads, full_len, HD)
        .transpose(0, 2, 1, 3)
        .reshape(clip_count, full_len, group_heads * HD)
    )
    token_attended = lax.all_to_all(
        attended, "ctx", split_axis=1, concat_axis=2, tiled=True
    ).reshape(row_count, local_width)
    attn_part = jnp.dot(token_attended, full_proj, preferred_element_type=jnp.float32)
    residual = inputs + tp_whole(attn_part) + out_shifts[0]
    normed_two_low = layer_norm(residual, norm_gains[1], norm_shifts[1]).astype(jnp.bfloat16)
    pre_act = jnp.dot(normed_two_low, full_up, preferred_element_type=jnp.float32) + b_up
    act_low = jax.nn.gelu(pre_act, approximate=False).astype(jnp.bfloat16)
    mlp_part = jnp.dot(act_low, full_down, preferred_element_type=jnp.float32)
    result = residual + tp_whole(mlp_part) + out_shifts[1]
    block_rows = result.astype(jnp.bfloat16)
    full_qkv, full_proj, full_up, full_down = (
        lax.all_gather(w_qkv, "fsdp", axis=1, tiled=True),
        lax.all_gather(w_proj, "fsdp", axis=1, tiled=True),
        lax.all_gather(w_up, "fsdp", axis=0, tiled=True),
        lax.all_gather(w_down, "fsdp", axis=1, tiled=True),
    )
    upstream = grad_out.reshape(row_count, width).astype(jnp.float32)
    upstream_low = upstream.astype(jnp.bfloat16)
    grad_down = contract_rows(act_low, upstream_low)
    grad_act = contract_cols(upstream_low, full_down)
    _, gelu_pull = jax.vjp(partial(jax.nn.gelu, approximate=False), pre_act)
    grad_pre = gelu_pull(grad_act)[0].astype(jnp.bfloat16)
    grad_b_up = jnp.sum(grad_pre.astype(jnp.float32), axis=0)
    grad_up = contract_rows(normed_two_low, grad_pre)
    back_part_two = contract_cols(grad_pre, full_up)
    grad_normed_two = tp_whole(back_part_two)
    _, norm_pull_two = jax.vjp(layer_norm, residual, norm_gains[1], norm_shifts[1])
    grad_res_norm, grad_gain_two, grad_shift_two = norm_pull_two(grad_normed_two)
    grad_residual = upstream + grad_res_norm
    grad_residual_low = grad_residual.astype(jnp.bfloat16)
    grad_proj = contract_rows(token_attended, grad_residual_low)
    grad_token_att = (
        contract_cols(grad_residual_low, full_proj)
        .astype(jnp.bfloat16)
        .reshape(clip_count, local_len, local_width)
    )
    grad_head_att = lax.all_to_all(grad_token_att, "ctx", split_axis=2, concat_axis=1, tiled=True)
    grad_grouped = (
        grad_head_att.reshape(clip_count, full_len, group_heads, HD)
        .transpose(0, 2, 1, 3)
        .reshape(group_count, full_len, HD)
    )
    grad_q, grad_k, grad_v = lax.map(
        backward_group, (grouped[0], grouped[1], grouped[2], grad_grouped, log_totals)
    )
    grad_heads = jnp.stack([grad_q, grad_k, grad_v]).astype(jnp.bfloat16)
    grad_heads = (
        grad_heads.reshape(3, clip_count, group_heads, full_len, HD)
        .transpose(0, 1, 3, 2, 4)
        .reshape(3, clip_count, full_len, group_heads * HD)
    )
    grad_tokens = (
        lax.all_to_all(grad_heads, "ctx", split_axis=2, concat_axis=3, tiled=True)
        .reshape(3, row_count, local_width)
        .astype(jnp.float32)
    )

    def rotate_rows(moved):
        return rotary(moved, cos_table, sin_table)

    _, rotary_pull = jax.vjp(rotate_rows, jnp.zeros(head_shape, jnp.float32))
    grad_q_pre = rotary_pull(grad_tokens[0].reshape(head_shape))[0].reshape(row_count, local_width)
    grad_k_pre = rotary_pull(grad_tokens[1].reshape(head_shape))[0].reshape(row_count, local_width)
    grad_qkv_low = jnp.stack([grad_q_pre, grad_k_pre, grad_tokens[2]]).astype(jnp.bfloat16)
    grad_b_qkv = jnp.sum(grad_qkv_low.astype(jnp.float32), axis=1)
    grad_qkv = jnp.einsum(
        "rd,cre->cde", normed_one_low, grad_qkv_low, preferred_element_type=jnp.float32
    )
    back_part_one = jnp.einsum(
        "cre,cde->rd", grad_qkv_low, full_qkv, preferred_element_type=jnp.float32
    )
    grad_normed_one = tp_whole(back_part_one)
    _, norm_pull_one = jax.vjp(layer_norm, inputs, norm_gains[0], norm_shifts[0])
    grad_in_norm, grad_gain_one, grad_shift_one = norm_pull_one(grad_normed_one)
    grad_input_rows = grad_residual + grad_in_norm
    norm_vectors = jnp.stack(
        [
            grad_gain_one,
            grad_gain_two,
            grad_shift_one,
            grad_shift_two,
            jnp.sum(grad_residual, axis=0),
            jnp.sum(upstream, axis=0),
        ]
    )
    block_output = block_rows.reshape(clip_count, local_len, width)
    grad_input = grad_input_rows.reshape(clip_count, local_len, width)
    shard_qkv, shard_proj, shard_up, shard_down = (
        lax.psum_scatter(
            grad_qkv.astype(jnp.bfloat16), "fsdp", scatter_dimension=1, tiled=True
        ).astype(jnp.float32),
        lax.psum_scatter(
            grad_proj.astype(jnp.bfloat16), "fsdp", scatter_dimension=1, tiled=True
        ).astype(jnp.float32),
        lax.psum_scatter(
            grad_up.astype(jnp.bfloat16), "fsdp", scatter_dimension=0, tiled=True
        ).astype(jnp.float32),
        lax.psum_scatter(
            grad_down.astype(jnp.bfloat16), "fsdp", scatter_dimension=1, tiled=True
        ).astype(jnp.float32),
    )
    shard_qkv, shard_proj, shard_up, shard_down = (
        lax.psum(shard_qkv.astype(jnp.bfloat16), "ctx").astype(jnp.float32),
        lax.psum(shard_proj.astype(jnp.bfloat16), "ctx").astype(jnp.float32),
        lax.psum(shard_up.astype(jnp.bfloat16), "ctx").astype(jnp.float32),
        lax.psum(shard_down.astype(jnp.bfloat16), "ctx").astype(jnp.float32),
    )
    gains_sum, shifts_sum, outs_sum, bqkv_sum, bup_sum = lax.psum(
        (norm_vectors[0:2], norm_vectors[2:4], norm_vectors[4:6], grad_b_qkv, grad_b_up),
        ("fsdp", "ctx"),
    )
    return (
        block_output,
        grad_input,
        shard_qkv,
        bqkv_sum,
        shard_proj,
        shard_up,
        bup_sum,
        shard_down,
        gains_sum,
        shifts_sum,
        outs_sum,
    )


def solution(mesh):
    in_specs = (
        P("fsdp", "ctx", None),
        P(None, "fsdp", "ctx"),
        P(None, "fsdp", "tp"),
        P(None, "tp"),
        P("tp", "fsdp"),
        P("fsdp", "tp"),
        P("tp"),
        P("tp", "fsdp"),
        P(),
        P(),
        P(),
        P("fsdp", "ctx", None),
    )
    out_specs = (
        P("fsdp", "ctx", None),
        P("fsdp", "ctx", None),
        P(None, "fsdp", "tp"),
        P(None, "tp"),
        P("tp", "fsdp"),
        P("fsdp", "tp"),
        P("tp"),
        P("tp", "fsdp"),
        P(),
        P(),
        P(),
    )
    return jax.shard_map(shards, mesh=mesh, in_specs=in_specs, out_specs=out_specs, check_vma=False)
```

profile of v0, /device:TPU:0, one launch (start us, length us, event | category | flops | bytes accessed | tf_op | source)
XLA Modules:
  0.0 875.1 jit_solution(13437522062420596701)
XLA Ops:
  7.3 2.4 copy.73
  9.7 1.9 convert_reduce_fusion.2
  15.1 2.1 fusion.40
  17.3 22.8 %all-gather.4.cloned.1.call-done = bf16[3,1024,256]{1,2,0:T(8,128)(2,1)} async-done(((bf16[3,512,256]{1,2,0:T(8,128)(2,1)}), bf16[3,1024,256]{1,2,0:T(8,128)(2,1)}) %all-gather.4.cloned.1.call-update) | async-done | bytes 1572880 | tf_op jit(solution)/shard_map/all_gather | solution.py:137
  40.1 3.9 add_bitcast_fusion
  46.6 2.1 concatenate.14
  49.0 2.1 concatenate.13
  51.5 3.1 pad_maximum_fusion.1
  54.5 3.8 all-to-all-start
  58.3 20.0 %all-to-all-done = bf16[3,2,512,256]{2,1,0,3:T(2,128)(2,1)S(1)} async-done(((bf16[3,2,512,256]{2,1,0,3:T(2,128)(2,1)}), bf16[3,2,512,256]{2,1,0,3:T(2,128)(2,1)S(1)}, u32[]{:S(2)}, u32[]{:S(2)}) %all-to-all-start) | async-done | bytes 1572896 | tf_op jit(solution)/shard_map/all_to_all | solution.py:161
  83.0 27.2 %while.54 = (s32[]{:T(128)}, bf16[2,4,512,64]{2,3,1,0:T(8,128)(2,1)}, f32[2,4,512]{2,1,0:T(4,128)S(1)}, bf16[2,2048,64]{2,1,0:T(8,128)(2,1)S(1)}, bf16[2,2048,64...) while((s32[]{:T(128)}, ...), condition=%wide.region_7.8_spmd, body=%wide.region_2.7_spmd.sunk | while | flops 277904896 | bytes 20156772 | solution.py:168
  84.4 11.4 %while.57 = (s32[]{:T(128)}, bf16[4,512,64]{1,2,0:T(8,128)(2,1)S(1)}, f32[4,512]{1,0:T(4,128)S(1)}, bf16[4,512,64]{2,1,0:T(8,128)(2,1)S(1)}, bf16[2048,64]{1,0:T...) while((s32[]{:T(128)}, bf16[4,512,64]{1,2,0:T(8,128)(2,1)S(1)}, ...), condition=%wide.region_6.6_spmd, body=%wide.region_3.5_spmd.sunk | while | flops 277904896 | bytes 13848681 | solution.py:76
  98.0 11.4 %while.57 = (s32[]{:T(128)}, bf16[4,512,64]{1,2,0:T(8,128)(2,1)S(1)}, f32[4,512]{1,0:T(4,128)S(1)}, bf16[4,512,64]{2,1,0:T(8,128)(2,1)S(1)}, bf16[2048,64]{1,0:T...) while((s32[]{:T(128)}, bf16[4,512,64]{1,2,0:T(8,128)(2,1)S(1)}, ...), condition=%wide.region_6.6_spmd, body=%wide.region_3.5_spmd.sunk | while | flops 277904896 | bytes 13848681 | solution.py:76
  110.3 2.6 copy.101
  114.4 3.5 all-to-all-start.1
  117.9 9.3 %all_gather.17 = bf16[256,1024]{1,0:T(8,128)(2,1)S(1)} all-gather(bf16[256,512]{1,0:T(8,128)(2,1)S(1)} %copy-done.30), channel_id=1, replica_groups=mesh['fsdp'=2,'ctx'=4,'tp'=4] {'fsdp'}, dimensions={1}, use_global_device_ids=true | all-gather | bytes 786432 | tf_op jit(solution)/shard_map/all_gather | solution.py:138
  128.0 1.9 copy.82
  131.1 2.1 convolution_convert_fusion.4
  135.5 84.2 %all-reduce.22.cloned.1.call-done = bf16[1024,1024]{1,0:T(8,128)(2,1)} async-done(((bf16[1024,1024]{1,0:T(8,128)(2,1)}), bf16[1024,1024]{1,0:T(8,128)(2,1)}) %all-reduce.22.cloned.1.call-update) | async-done | bytes 2097168 | tf_op jit(solution)/shard_map/psum | solution.py:55
  219.7 2.5 fusion.50
  222.2 3.0 multiply_reduce_fusion.2
  225.3 28.2 %all-gather.6.cloned.1.call-done = bf16[1024,1024]{1,0:T(8,128)(2,1)} async-done(((bf16[512,1024]{1,0:T(8,128)(2,1)}), bf16[1024,1024]{1,0:T(8,128)(2,1)}) %all-gather.6.cloned.1.call-update) | async-done | bytes 2097168 | tf_op jit(solution)/shard_map/all_gather | solution.py:139
  253.4 7.4 fusion.69
  260.8 27.1 %all-gather.8.cloned.1.call-done = bf16[1024,1024]{1,0:T(8,128)(2,1)} async-done(((bf16[1024,512]{1,0:T(8,128)(2,1)}), bf16[1024,1024]{1,0:T(8,128)(2,1)}) %all-gather.8.cloned.1.call-update) | async-done | bytes 2097168 | tf_op jit(solution)/shard_map/all_gather | solution.py:140
  287.9 16.0 %convert_reduce_fusion.4 = (f32[1024]{0:T(1024)}, bf16[1024,1024]{1,0:T(8,128)(2,1)S(1)}, f32[1024,1024]{1,0:T(8,128)}) fusion(f32[1024,1024]{1,0:T(8,128)} %fusion.69, f32[1024]{0:T(1024)S(1)} %copy-done.50, bf16[1024,1024]{1,0:T(8,128)(2,1)S(1)} %bitcast.274, bf16[1024,1024]{1,0:T(8,128)(2,1)} %all-gather.8.cloned.1.call-done), kind=kOutput, calls=%fused_computation.82 | convolution fusion | flops 2226125824 | bytes 14688256 | tf_op jit(solution)/shard_map/dot_general | solution.py:49
  305.2 3.7 convolution_convert_fusion.2
  308.9 12.1 %reduce-scatter.7.cloned.1.call-start = ((), (), s32[]{:S(2)}) async-start(), calls=%async_computation.14 | async-start | bytes 786432 | tf_op jit(solution)/shard_map/reduce_scatter | solution.py:266
  321.1 74.2 %all-reduce.24.cloned.1.call-done = bf16[1024,1024]{1,0:T(8,128)(2,1)} async-done(((bf16[1024,1024]{1,0:T(8,128)(2,1)}), bf16[1024,1024]{1,0:T(8,128)(2,1)}) %all-reduce.24.cloned.1.call-update) | async-done | bytes 2097168 | tf_op jit(solution)/shard_map/psum | solution.py:55
  395.3 4.5 convert_reduce_fusion.1
  400.0 2.7 fusion.34
  402.7 2.4 fusion.70
  405.0 2.0 copy-done.3
  408.6 4.6 multiply_convert_fusion.1
  414.5 3.8 convolution_convert_fusion
  418.3 3.0 convolution_convert_fusion.6
  422.5 3.5 all-to-all-start.2
  426.0 6.9 convolution_convert_fusion.1
  433.0 1.8 all-to-all-done.2
  436.1 103.6 %while.56 = (s32[]{:T(128)}, bf16[2,2048,64]{2,0,1:T(2,128)(2,1)}, bf16[2,2048,64]{1,2,0:T(8,128)(2,1)}, bf16[2,2048,64]{1,2,0:T(8,128)(2,1)}, bf16[2,2048,64]{2...) while((s32[]{:T(128)}, bf16[2,2048,64]{2,0,1:T(2,128)(2,1)}, ...), condition=%wide.region_19.20_spmd, body=%wide.region_15.19_spmd.sunk | while | flops 680164864 | bytes 41838996 | solution.py:217
  440.5 20.1 %while.58 = (s32[]{:T(128)}, f32[2048,64]{0,1:T(8,128)S(1)}, f32[2048,64]{0,1:T(8,128)S(1)}, f32[4,512,64]{1,2,0:T(8,128)}, bf16[4,512,64]{2,1,0:T(8,128)(2,1)S(...) while((s32[]{:T(128)}, f32[2048,64]{0,1:T(8,128)S(1)}, ...), condition=%wide.region_18.18_spmd.clone, body=%wide.region_16.17_spmd.clone.sunk | while | flops 680164864 | bytes 35530900 | solution.py:111
  462.0 25.1 %dynamic_update_slice.47 = bf16[2,2048,64]{2,0,1:T(2,128)(2,1)} dynamic-update-slice(bf16[2,2048,64]{2,0,1:T(2,128)(2,1)} %get-tuple-element.795, f32[1,2048,64]{2,0,1:T(1,128)S(1)} %bitcast.268, s32[]{:T(128)S(6)} %copy.189, s32[]{:T(128)} %constant.78.clone.1..sunk.2, s32[]{:T(128)} %constant.78.clone.1..sunk.2) | dynamic-update-slice | bytes 1048580 | tf_op jit(solution)/shard_map/while/body/jit(dynamic_update_index_in_dim)/dynamic_update_slice | solution.py:217
  492.3 20.1 %while.58 = (s32[]{:T(128)}, f32[2048,64]{0,1:T(8,128)S(1)}, f32[2048,64]{0,1:T(8,128)S(1)}, f32[4,512,64]{1,2,0:T(8,128)}, bf16[4,512,64]{2,1,0:T(8,128)(2,1)S(...) while((s32[]{:T(128)}, f32[2048,64]{0,1:T(8,128)S(1)}, ...), condition=%wide.region_18.18_spmd.clone, body=%wide.region_16.17_spmd.clone.sunk | while | flops 680164864 | bytes 35530900 | solution.py:111
  513.8 25.1 %dynamic_update_slice.47 = bf16[2,2048,64]{2,0,1:T(2,128)(2,1)} dynamic-update-slice(bf16[2,2048,64]{2,0,1:T(2,128)(2,1)} %get-tuple-element.795, f32[1,2048,64]{2,0,1:T(1,128)S(1)} %bitcast.268, s32[]{:T(128)S(6)} %copy.189, s32[]{:T(128)} %constant.78.clone.1..sunk.2, s32[]{:T(128)} %constant.78.clone.1..sunk.2) | dynamic-update-slice | bytes 1048580 | tf_op jit(solution)/shard_map/while/body/jit(dynamic_update_index_in_dim)/dynamic_update_slice | solution.py:217
  539.7 3.6 copy.142
  543.3 3.6 copy.141
  546.8 7.2 fusion.79
  554.0 3.3 reshape.228
  557.3 24.7 %all_to_all.57 = bf16[4,2,98304]{2,1,0:T(2,128)(2,1)} all-to-all(bf16[4,2,98304]{2,1,0:T(2,128)(2,1)} %reshape.228), channel_id=1, replica_groups=mesh['fsdp'=2,'ctx'=4,'tp'=4] {'ctx'}, dimensions={0} | all-to-all | bytes 3145728 | tf_op jit(solution)/shard_map/all_to_all | solution.py:227
  582.0 3.8 reshape.229
  585.8 6.4 copy.92
  601.3 4.9 fusion.61
  606.3 5.4 convolution_convert_fusion.3
  611.7 3.1 bitcast_convert_fusion
  615.2 2.1 convert_reduce_fusion.3
  618.7 11.9 %reduce-scatter.5.cloned.1.call-done = bf16[3,512,256]{1,2,0:T(8,128)(2,1)} async-done(((bf16[3,1024,256]{1,2,0:T(8,128)(2,1)}), bf16[3,512,256]{1,2,0:T(8,128)(2,1)}) %reduce-scatter.5.cloned.1.call-update) | async-done | bytes 786448 | tf_op jit(solution)/shard_map/reduce_scatter | solution.py:263
  630.7 157.9 %all-reduce.26.cloned.1.call-done = (bf16[1024,1024]{1,0:T(8,128)(2,1)}, bf16[1024,1024]{1,0:T(8,128)(2,1)}) async-done(((bf16[1024,1024]{1,0:T(8,128)(2,1)}, bf16[1024,1024]{1,0:T(8,128)(2,1)}), (bf16[1024,1024]{1,0:T(8,128)(2,1)}, bf16[1024,1024]{1,0:T(8,128)(2,1)})) %all-reduce.26.cloned.1.call-update) | async-done | bytes 4194320 | tf_op jit(solution)/shard_map/psum | solution.py:55
  788.6 3.1 convert_reduce_fusion
  791.7 2.7 fusion.35
  794.5 26.2 %all-reduce.14 = (f32[3,256]{1,0:T(4,128)}, f32[1024]{0:T(1024)}, f32[2,1024]{1,0:T(2,128)}, f32[2,1024]{1,0:T(2,128)}, f32[2,1024]{1,0:T(2,128)}) all-reduce(f32[3,256]{1,0:T(4,128)S(1)} %convert_reduce_fusion.5, f32[1024]{0:T(1024)S(1)} %copy-done.52, ...), channel_id=1, replica_groups=mesh['fsdp'=2,'ctx'=4,'tp'=4] {'fsdp','ctx'}, use_global_device_ids=true, to_apply=%region_26.27 | all-reduce | flops 7936 | bytes 63488 | tf_op jit(solution)/shard_map/psum | solution.py:282
  820.7 7.1 add_add_fusion.2
  827.9 31.4 %all-reduce.28.cloned.1.call-done = (bf16[3,512,256]{1,2,0:T(8,128)(2,1)}, bf16[256,512]{1,0:T(8,128)(2,1)}, bf16[512,1024]{1,0:T(8,128)(2,1)}, bf16[1024,512]{1,0:T(8,128)(2,1)}) async-done(((bf16[3,512,256]{1,2,0:T(8,128)(2,1)}, bf16[256,512]{1,0:T(8,128)(2,1)}, bf16[512,1024]{1,0:T(8,128)(2,1)}, bf16[1024,512]{1,0:T(8,128)(2,1)}), (bf16[3,512,256]{1,2,0:T(8,128)(2,1)}, bf16[256,512]{1,0:T(8,128)(2,1)}, ...) | async-done | bytes 3145744 | tf_op jit(solution)/shard_map/psum | solution.py:277
  859.2 1.9 convert_element_type.168
  861.1 2.5 copy.98
  863.7 2.8 convert_element_type.170
  (335 shorter events, 116.5 us)
Async XLA Ops:
  7.2 4.5 copy-start
  7.2 5.3 copy-start.46
  7.2 5.8 copy-start.47
  7.2 6.4 copy-start.48
  7.2 32.9 %all-gather.4.cloned.1.call-start = ((), (), s32[]{:S(2)}) async-start(), calls=%async_computation.8 | async-start | bytes 2359296 | tf_op jit(solution)/shard_map/all_gather | solution.py:137
  11.7 28.4 %copy-start.55 = (f32[3,256]{1,0:T(4,128)S(1)}, f32[3,256]{1,0:T(4,128)}, u32[]{:S(2)}) copy-start(f32[3,256]{1,0:T(4,128)} %param.23) | copy-start | bytes 9220
  11.7 3.4 copy-start.31
  12.5 2.6 copy-start.38
  15.0 30.8 %copy-start.15 = (f32[1024,10]{0,1:T(8,128)}, f32[1024,10]{0,1:T(8,128)S(1)}, u32[]{:S(2)}) copy-start(f32[1024,10]{0,1:T(8,128)S(1)} %get-tuple-element.436) | copy-start | bytes 122884
  15.0 30.8 %copy-start.17 = (f32[1024,10]{0,1:T(8,128)}, f32[1024,10]{0,1:T(8,128)S(1)}, u32[]{:S(2)}) copy-start(f32[1024,10]{0,1:T(8,128)S(1)} %get-tuple-element.437) | copy-start | bytes 122884
  15.0 30.8 %copy-start.19 = (f32[1024,10]{0,1:T(8,128)}, f32[1024,10]{0,1:T(8,128)S(1)}, u32[]{:S(2)}) copy-start(f32[1024,10]{0,1:T(8,128)S(1)} %get-tuple-element.438) | copy-start | bytes 122884
  15.1 30.8 %copy-start.21 = (f32[1024,10]{0,1:T(8,128)}, f32[1024,10]{0,1:T(8,128)S(1)}, u32[]{:S(2)}) copy-start(f32[1024,10]{0,1:T(8,128)S(1)} %get-tuple-element.449) | copy-start | bytes 122884
  15.1 30.8 %copy-start.23 = (f32[1024,10]{0,1:T(8,128)}, f32[1024,10]{0,1:T(8,128)S(1)}, u32[]{:S(2)}) copy-start(f32[1024,10]{0,1:T(8,128)S(1)} %get-tuple-element.450) | copy-start | bytes 122884
  15.1 30.8 %copy-start.25 = (f32[1024,10]{0,1:T(8,128)}, f32[1024,10]{0,1:T(8,128)S(1)}, u32[]{:S(2)}) copy-start(f32[1024,10]{0,1:T(8,128)S(1)} %get-tuple-element.451) | copy-start | bytes 122884
  54.5 23.8 %all-to-all-start = ((bf16[3,2,512,256]{2,1,0,3:T(2,128)(2,1)}), bf16[3,2,512,256]{2,1,0,3:T(2,128)(2,1)S(1)}, u32[]{:S(2)}, u32[]{:S(2)}) async-start(bf16[3,2,512,256]{2,1,0,3:T(2,128)(2,1)} %pad_maximum_fusion.1), calls=%async_computation | async-start | bytes 3145728 | tf_op jit(solution)/shard_map/all_to_all | solution.py:161
  84.4 11.4 %copy-start.28 = (bf16[2,4,512,64]{2,3,1,0:T(8,128)(2,1)S(1)}, bf16[2,4,512,64]{2,3,1,0:T(8,128)(2,1)}, u32[]{:S(2)}) copy-start(bf16[2,4,512,64]{2,3,1,0:T(8,128)(2,1)} %get-tuple-element.762) | copy-start | bytes 1572868 | tf_op jit(solution)/shard_map/while
  98.0 11.4 %copy-start.28 = (bf16[2,4,512,64]{2,3,1,0:T(8,128)(2,1)S(1)}, bf16[2,4,512,64]{2,3,1,0:T(8,128)(2,1)}, u32[]{:S(2)}) copy-start(bf16[2,4,512,64]{2,3,1,0:T(8,128)(2,1)} %get-tuple-element.762) | copy-start | bytes 1572868 | tf_op jit(solution)/shard_map/while
  110.2 19.6 %copy-start.5 = (bf16[2,2048,64]{2,1,0:T(8,128)(2,1)}, bf16[2,2048,64]{2,1,0:T(8,128)(2,1)S(1)}, u32[]{:S(2)}) copy-start(bf16[2,2048,64]{2,1,0:T(8,128)(2,1)S(1)} %get-tuple-element.841) | copy-start | bytes 1572868
  110.3 7.7 copy-start.30
  114.4 12.8 %all-to-all-start.1 = ((bf16[4,2,32768]{2,1,0:T(2,128)(2,1)}), bf16[4,2,32768]{2,1,0:T(2,128)(2,1)S(1)}, u32[]{:S(2)}, u32[]{:S(2)}) async-start(bf16[4,2,32768]{2,1,0:T(2,128)(2,1)} %reshape.226), calls=%async_computation.1 | async-start | bytes 1048576 | tf_op jit(solution)/shard_map/all_to_all | solution.py:174
  117.9 101.8 %all-reduce.22.cloned.1.call-start = ((), (), s32[]{:S(2)}) async-start(), calls=%async_computation.9 | async-start | bytes 4194304 | tf_op jit(solution)/shard_map/psum | solution.py:55
  129.9 5.0 copy-start.49
  129.9 89.8 %copy-start.1 = (bf16[2,512,1024]{2,1,0:T(8,128)(2,1)S(1)}, bf16[2,512,1024]{2,1,0:T(8,128)(2,1)}, u32[]{:S(2)}) copy-start(bf16[2,512,1024]{2,1,0:T(8,128)(2,1)} %param.20) | copy-start | bytes 6291460
  133.2 120.2 %all-gather.6.cloned.1.call-start = ((), (), s32[]{:S(2)}) async-start(), calls=%async_computation.10 | async-start | bytes 3145728 | tf_op jit(solution)/shard_map/all_gather | solution.py:139
  134.0 154.0 %all-gather.8.cloned.1.call-start = ((), (), s32[]{:S(2)}) async-start(), calls=%async_computation.11 | async-start | bytes 3145728 | tf_op jit(solution)/shard_map/all_gather | solution.py:140
  134.5 260.7 %all-reduce.24.cloned.1.call-start = ((), (), s32[]{:S(2)}) async-start(), calls=%async_computation.12 | async-start | bytes 4194304 | tf_op jit(solution)/shard_map/psum | solution.py:55
  135.5 89.7 %copy-start.36 = (f32[1,1024]{1,0:T(1,128)}, f32[1,1024]{1,0:T(1,128)S(1)}, u32[]{:S(2)}) copy-start(f32[1,1024]{1,0:T(1,128)S(1)} %get-tuple-element.442) | copy-start | bytes 12292
  219.7 2.5 copy-start.6
  222.2 31.2 %copy-start.35 = (f32[1,1024]{1,0:T(1,128)S(1)}, f32[1,1024]{1,0:T(1,128)}, u32[]{:S(2)}) copy-start(f32[1,1024]{1,0:T(1,128)} %get-tuple-element.443) | copy-start | bytes 12292
  222.2 31.2 %copy-start.51 = (f32[1,1024]{1,0:T(1,128)S(1)}, f32[1,1024]{1,0:T(1,128)}, u32[]{:S(2)}) copy-start(f32[1,1024]{1,0:T(1,128)} %get-tuple-element.445) | copy-start | bytes 12292
  253.4 34.5 %copy-start.10 = (bf16[2,512,1024]{2,1,0:T(8,128)(2,1)S(1)}, bf16[2,512,1024]{2,1,0:T(8,128)(2,1)}, u32[]{:S(2)}) copy-start(bf16[2,512,1024]{2,1,0:T(8,128)(2,1)} %param.31) | copy-start | bytes 6291460
  253.4 34.5 %copy-start.50 = (f32[1024]{0:T(1024)S(1)}, f32[1024]{0:T(1024)}, u32[]{:S(2)}) copy-start(f32[1024]{0:T(1024)} %param.26) | copy-start | bytes 12292
  287.9 17.3 %copy-start.53 = (bf16[1024,1024]{1,0:T(8,128)(2,1)S(1)}, bf16[1024,1024]{1,0:T(8,128)(2,1)}, u32[]{:S(2)}) copy-start(bf16[1024,1024]{1,0:T(8,128)(2,1)} %all-gather.6.cloned.1.call-done) | copy-start | bytes 6291460
  308.9 309.7 %reduce-scatter.7.cloned.1.call-start = ((), (), s32[]{:S(2)}) async-start(), calls=%async_computation.14 | async-start | bytes 786432 | tf_op jit(solution)/shard_map/reduce_scatter | solution.py:266
  395.2 4.5 copy-start.4
  395.3 4.7 copy-start.7
  405.0 2.0 copy-start.3
  408.5 210.2 %reduce-scatter.11.cloned.1.call-start = ((), (), s32[]{:S(2)}) async-start(), calls=%async_computation.16 | async-start | bytes 3145728 | tf_op jit(solution)/shard_map/reduce_scatter | solution.py:272
  422.5 12.3 %all-to-all-start.2 = ((bf16[2,512,256]{1,0,2:T(2,128)(2,1)}), bf16[2,512,256]{1,0,2:T(2,128)(2,1)S(1)}, u32[]{:S(2)}, u32[]{:S(2)}) async-start(bf16[2,512,256]{1,0,2:T(2,128)(2,1)} %copy.83), calls=%async_computation.2 | async-start | bytes 1048576 | tf_op jit(solution)/shard_map/all_to_all | solution.py:211
  426.0 192.7 %reduce-scatter.9.cloned.1.call-start = ((), (), s32[]{:S(2)}) async-start(), calls=%async_computation.15 | async-start | bytes 3145728 | tf_op jit(solution)/shard_map/reduce_scatter | solution.py:269
  432.9 197.7 %reduce-scatter.5.cloned.1.call-start = ((), (), s32[]{:S(2)}) async-start(), calls=%async_computation.13 | async-start | bytes 2359296 | tf_op jit(solution)/shard_map/reduce_scatter | solution.py:263
  592.2 2.9 copy-start.9
  596.4 1.7 copy-start.16
  596.4 1.7 copy-start.18
  596.4 1.7 copy-start.20
  598.9 2.4 copy-start.13
  601.3 5.0 copy-start.12
  606.2 182.3 %all-reduce.26.cloned.1.call-start = ((), (), s32[]{:S(2)}) async-start(), calls=%async_computation.17 | async-start | bytes 8388608 | tf_op jit(solution)/shard_map/psum | solution.py:55
  606.3 5.4 copy-start.14
  606.3 5.4 copy-start.54
  614.8 2.5 copy-start.42
  614.8 173.7 %copy-start.2 = (bf16[2,512,1024]{2,1,0:T(8,128)(2,1)S(1)}, bf16[2,512,1024]{2,1,0:T(8,128)(2,1)}, u32[]{:S(2)}) copy-start(bf16[2,512,1024]{2,1,0:T(8,128)(2,1)} %param.20) | copy-start | bytes 6291460
  614.8 173.7 %copy-start.32 = (f32[1,4,2,128]{3,1,2,0:T(4,128)S(1)}, f32[1,4,2,128]{3,1,2,0:T(4,128)}, u32[]{:S(2)}) copy-start(f32[1,4,2,128]{3,1,2,0:T(4,128)} %copy-done.31) | copy-start | bytes 12292
  614.9 173.7 %copy-start.34 = (f32[1,1024]{1,0:T(1,128)S(1)}, f32[1,1024]{1,0:T(1,128)}, u32[]{:S(2)}) copy-start(f32[1,1024]{1,0:T(1,128)} %copy-done.33) | copy-start | bytes 12292
  614.9 244.4 %all-reduce.28.cloned.1.call-start = ((), (), s32[]{:S(2)}) async-start(), calls=%async_computation.18 | async-start | bytes 6291456 | tf_op jit(solution)/shard_map/psum | solution.py:277
  617.3 174.4 %copy-start.41 = (f32[1,4,2,128]{3,1,2,0:T(4,128)S(1)}, f32[1,4,2,128]{3,1,2,0:T(4,128)}, u32[]{:S(2)}) copy-start(f32[1,4,2,128]{3,1,2,0:T(4,128)} %copy-done.40) | copy-start | bytes 12292
  617.3 174.4 %copy-start.44 = (f32[1024]{0:T(1024)S(1)}, f32[1024]{0:T(1024)}, u32[]{:S(2)}) copy-start(f32[1024]{0:T(1024)} %get-tuple-element.296) | copy-start | bytes 12292
  617.3 174.4 %copy-start.39 = (f32[1024]{0:T(1024)S(1)}, f32[1024]{0:T(1024)}, u32[]{:S(2)}) copy-start(f32[1024]{0:T(1024)} %copy-done.38) | copy-start | bytes 12292
  788.5 3.2 copy-start.8
  788.5 5.9 copy-start.43
  788.5 5.9 copy-start.52
  788.6 32.2 %copy-start.37 = (f32[1,1024]{1,0:T(1,128)S(1)}, f32[1,1024]{1,0:T(1,128)}, u32[]{:S(2)}) copy-start(f32[1,1024]{1,0:T(1,128)} %copy-done.36) | copy-start | bytes 12292
  788.6 32.2 %copy-start.45 = (f32[1,1024]{1,0:T(1,128)S(1)}, f32[1,1024]{1,0:T(1,128)}, u32[]{:S(2)}) copy-start(f32[1,1024]{1,0:T(1,128)} %get-tuple-element.441) | copy-start | bytes 12292
  859.2 7.2 copy-start.27
  (9 other events, 11.5 us)
Sparse Core Ops, SparseCore 0:
  10.1 29.8 all-gather.3
  133.3 86.3 all-reduce.21
  221.2 32.1 all-gather.5
  254.8 33.0 all-gather.7
  309.1 86.1 all-reduce.23
  408.7 13.6 reduce-scatter.6
  424.6 31.8 reduce-scatter.10
  458.8 31.8 reduce-scatter.8
  606.3 24.2 reduce-scatter.4
  633.5 155.0 all-reduce.25
  791.1 68.0 all-reduce.27
where the time goes:
time: 888 us; the launch traced here: 875 us
  waiting for transfers between devices  461 us (52%)
  local copies, waits for them, and re-layouts  130 us (15%)
  matrix products  113 us (13%)
  other arithmetic  71.1 us (8%)
  blocking collectives  60.2 us (7%)
  starting transfers between devices  23.8 us (3%)
  between operations  15.3 us (2%)
    psum x3, waiting for transfers between devices, tp_whole(): return lax.psum(partial_sum.astype(jnp.bfloat16), 'tp').astype(jnp.float32)  316 us
    dynamic_update_slice x4, local copies, waits for them, and re-layouts, shards(): lax.map(backward_group, (grouped[0], grouped[1], grouped[2], grad_grouped...  51.9 us
    psum x1, waiting for transfers between devices, shards(): lax.psum(shard_qkv.astype(jnp.bfloat16), 'ctx').astype(jnp.float32)  31.4 us
    unnamed x122, local copies, waits for them, and re-layouts  28.2 us
    all_gather x1, waiting for transfers between devices, shards(): lax.all_gather(w_up, 'fsdp', axis=0, tiled=True)  28.2 us
    all_gather x1, waiting for transfers between devices, shards(): lax.all_gather(w_down, 'fsdp', axis=1, tiled=True)  27.1 us
    psum x1, blocking collectives, shards(): lax.psum((norm_vectors[0:2], norm_vectors[2:4], norm_vectors[4:6], grad_b...  26.2 us
    all_to_all x1, blocking collectives, shards(): lax.all_to_all(grad_heads, 'ctx', split_axis=2, concat_axis=3, tiled=True)  24.7 us
  transfers between devices with their start and end apart: 14, of which 10 were waited for; matrix products, arithmetic and copies ran while one was open for 24% of the time, Pallas kernels for 0%

commit v1 on v0

--- a/solution.py
+++ b/solution.py
@@ -9,6 +9,26 @@
 ROT = 20
 QBLK = 512
 EPSILON = 1e-06
+
+
+def _run_knots(w_in, on_dim):
+    w_in = jnp.moveaxis(w_in, 0, on_dim)
+    oldest = w_in.shape
+    return w_in.reshape(
+        *oldest[:on_dim], oldest[on_dim] * oldest[on_dim + 1], *oldest[on_dim + 2 :]
+    )
+
+
+def _feed_routes_all(z, group_axis):
+    devs = jax.lax.axis_size(group_axis)
+    y = z[None]
+    for p in range(devs.bit_length() - 1):
+        base_arr = 1 << p
+        response = jax.lax.ppermute(y, group_axis, [(i0, i0 ^ base_arr) for i0 in range(devs)])
+        row_out = jnp.stack([y, response], axis=0)
+        wide_out = jax.lax.axis_index(group_axis) >> p & 1
+        y = jnp.where(wide_out == 0, row_out, row_out[::-1]).reshape(-1, *z.shape)
+    return y
 
 
 def layer_norm(values, gain_vec, shift_vec):
@@ -133,8 +153,12 @@
     group_heads = local_width // ctx_count // HD
     group_count = clip_count * group_heads
     inputs = block_input.reshape(row_count, width).astype(jnp.float32)
+
+    def read_pieces_all_up(where_dim, page, block_in):
+        return _run_knots(_feed_routes_all(block_in, page), where_dim)
+
     full_qkv, full_proj, full_up, full_down = (
-        lax.all_gather(w_qkv, "fsdp", axis=1, tiled=True),
+        read_pieces_all_up(1, "fsdp", w_qkv),
         lax.all_gather(w_proj, "fsdp", axis=1, tiled=True),
         lax.all_gather(w_up, "fsdp", axis=0, tiled=True),
         lax.all_gather(w_down, "fsdp", axis=1, tiled=True),

time: 888 us -> 808 us (0.910)
  waiting for transfers between devices: 461 us -> 415 us
  blocking collectives: 60.2 us -> 35 us
    all_gather x1, waiting for transfers between devices: 28.2 us -> 0.03 us  [shards(): lax.all_gather(w_up, 'fsdp', axis=0, tiled=True)]
    all_gather x1, waiting for transfers between devices: 27.1 us -> 0.01 us  [shards(): lax.all_gather(w_down, 'fsdp', axis=1, tiled=True)]
    all_to_all x1 -> x0, blocking collectives: 24.7 us -> none  [shards(): lax.all_to_all(grad_heads, 'ctx', split_axis=2, concat_axis=3, tiled=True)]
    all_gather x1, waiting for transfers between devices: 22.8 us -> 0.03 us  [shards(): lax.all_gather(w_qkv, 'fsdp', axis=1, tiled=True)]
    reduce_scatter x1, waiting for transfers between devices: 11.9 us -> 25 us  [shards(): lax.psum_scatter(grad_qkv.astype(jnp.bfloat16), 'fsdp', scatter_dimension...]
    reduce_scatter x1, starting transfers between devices: 12.1 us -> 0.04 us  [shards(): lax.psum_scatter(grad_proj.astype(jnp.bfloat16), 'fsdp', scatter_dimensio...]
    all_to_all x0 -> x1, waiting for transfers between devices: none -> 9.55 us  [shards(): lax.all_to_all(grad_heads, 'ctx', split_axis=2, concat_axis=3, tiled=True)]
    ppermute x0 -> x1, waiting for transfers between devices: none -> 9.37 us  [_feed_routes_all(): jax.lax.ppermute(y, group_axis, [(i0, i0 ^ base_arr) for i0 in range(devs)])]
  transfers between devices with their start and end apart: 14 -> 16, of which waited for: 10 -> 9; matrix products, arithmetic and copies ran while one was open for 24% -> 11% of each run, Pallas kernels for 0% -> 0%
where the time goes in v1:
time: 808 us; the launch traced here: 794 us
  waiting for transfers between devices  415 us (51%)
  local copies, waits for them, and re-layouts  123 us (15%)
  matrix products  111 us (14%)
  other arithmetic  73.4 us (9%)
  blocking collectives  35 us (4%)
  starting transfers between devices  19.2 us (2%)
  between operations  17 us (2%)
    psum x3, waiting for transfers between devices, tp_whole(): return lax.psum(partial_sum.astype(jnp.bfloat16), 'tp').astype(jnp.float32)  307 us
    dynamic_update_slice x4, local copies, waits for them, and re-layouts, shards(): lax.map(backward_group, (grouped[0], grouped[1], grouped[2], grad_grouped...  51.9 us
    psum x1, waiting for transfers between devices, shards(): lax.psum(shard_qkv.astype(jnp.bfloat16), 'ctx').astype(jnp.float32)  33.1 us
    unnamed x139, local copies, waits for them, and re-layouts  25.9 us
    psum x1, blocking collectives, shards(): lax.psum((norm_vectors[0:2], norm_vectors[2:4], norm_vectors[4:6], grad_b...  25.7 us
    dot_general x19, matrix products, contract_rows(): lax.dot_general(left_mat, right_mat, (((0,), (0,)), ((), ())), preferred_...  25.1 us
    reduce_scatter x1, waiting for transfers between devices, shards(): lax.psum_scatter(grad_qkv.astype(jnp.bfloat16), 'fsdp', scatter_dimension...  25 us
    dot_general x3, matrix products, contract_cols(): lax.dot_general(left_mat, right_mat, (((1,), (1,)), ((), ())), preferred_...  20.8 us
  transfers between devices with their start and end apart: 16, of which 9 were waited for; matrix products, arithmetic and copies ran while one was open for 11% of the time, Pallas kernels for 0%

profile of v1, /device:TPU:0, one launch (start us, length us, event | category | flops | bytes accessed | tf_op | source)
XLA Modules:
  0.0 794.1 jit_solution(12692247597143020800)
XLA Ops:
  8.1 3.1 collective-permute-start
  11.1 1.9 convert_reduce_fusion.2
  13.7 2.3 fusion.43
  19.5 9.4 %collective-permute-done = bf16[1,3,512,256]{3,2,1,0:T(8,128)(2,1)S(1)} collective-permute-done((bf16[1,3,512,256]{3,2,1,0:T(8,128)(2,1)}, bf16[1,3,512,256]{3,2,1,0:T(8,128)(2,1)S(1)}, u32[]{:S(2)}, u32[]{:S(2)}) %collective-permute-start) | collective-permute-done | bytes 786464 | tf_op jit(solution)/shard_map/ppermute | solution.py:27
  29.4 1.9 add_bitcast_fusion
  36.1 3.1 pad_maximum_fusion.2
  39.2 3.8 all-to-all-start
  43.0 20.0 %all-to-all-done = bf16[3,2,512,256]{2,1,0,3:T(2,128)(2,1)S(1)} async-done(((bf16[3,2,512,256]{2,1,0,3:T(2,128)(2,1)}), bf16[3,2,512,256]{2,1,0,3:T(2,128)(2,1)S(1)}, u32[]{:S(2)}, u32[]{:S(2)}) %all-to-all-start) | async-done | bytes 1572896 | tf_op jit(solution)/shard_map/all_to_all | solution.py:185
  67.6 27.2 %while.54 = (s32[]{:T(128)}, bf16[2,4,512,64]{2,3,1,0:T(8,128)(2,1)}, f32[2,4,512]{2,1,0:T(4,128)S(1)}, bf16[2,2048,64]{2,1,0:T(8,128)(2,1)S(1)}, bf16[2,2048,64...) while((s32[]{:T(128)}, ...), condition=%wide.region_7.8_spmd, body=%wide.region_2.7_spmd.sunk | while | flops 277904896 | bytes 20156772 | solution.py:192
  69.0 11.4 %while.57 = (s32[]{:T(128)}, bf16[4,512,64]{1,2,0:T(8,128)(2,1)S(1)}, f32[4,512]{1,0:T(4,128)S(1)}, bf16[4,512,64]{2,1,0:T(8,128)(2,1)S(1)}, bf16[2048,64]{1,0:T...) while((s32[]{:T(128)}, bf16[4,512,64]{1,2,0:T(8,128)(2,1)S(1)}, ...), condition=%wide.region_6.6_spmd, body=%wide.region_3.5_spmd.sunk | while | flops 277904896 | bytes 13848681 | solution.py:96
  82.6 11.4 %while.57 = (s32[]{:T(128)}, bf16[4,512,64]{1,2,0:T(8,128)(2,1)S(1)}, f32[4,512]{1,0:T(4,128)S(1)}, bf16[4,512,64]{2,1,0:T(8,128)(2,1)S(1)}, bf16[2048,64]{1,0:T...) while((s32[]{:T(128)}, bf16[4,512,64]{1,2,0:T(8,128)(2,1)S(1)}, ...), condition=%wide.region_6.6_spmd, body=%wide.region_3.5_spmd.sunk | while | flops 277904896 | bytes 13848681 | solution.py:96
  94.8 2.6 copy.96
  97.4 1.6 reshape.256
  99.0 3.5 all-to-all-start.1
  102.5 9.3 %all_gather.15 = bf16[256,1024]{1,0:T(8,128)(2,1)S(1)} all-gather(bf16[256,512]{1,0:T(8,128)(2,1)S(1)} %copy-done.36), channel_id=1, replica_groups=mesh['fsdp'=2,'ctx'=4,'tp'=4] {'fsdp'}, dimensions={1}, use_global_device_ids=true | all-gather | bytes 786432 | tf_op jit(solution)/shard_map/all_gather | solution.py:162
  114.3 2.1 convolution_convert_fusion.4
  118.2 86.1 %all-reduce.22.cloned.1.call-done = bf16[1024,1024]{1,0:T(8,128)(2,1)} async-done(((bf16[1024,1024]{1,0:T(8,128)(2,1)}), bf16[1024,1024]{1,0:T(8,128)(2,1)}) %all-reduce.22.cloned.1.call-update) | async-done | bytes 2097168 | tf_op jit(solution)/shard_map/psum | solution.py:75
  204.3 2.5 fusion.54
  206.8 3.0 multiply_reduce_fusion.2
  209.9 7.4 fusion.71
  217.3 16.4 %convert_reduce_fusion.4 = (f32[1024]{0:T(1024)}, bf16[1024,1024]{1,0:T(8,128)(2,1)S(1)}, f32[1024,1024]{1,0:T(8,128)}) fusion(f32[1024,1024]{1,0:T(8,128)} %fusion.71, f32[1024]{0:T(1024)S(1)} %copy-done.57, bf16[1024,1024]{1,0:T(8,128)(2,1)S(1)} %bitcast.282, bf16[1024,1024]{1,0:T(8,128)(2,1)} %all-gather.6.cloned.1.call-done), kind=kOutput, calls=%fused_computation.86 | convolution fusion | flops 2226125824 | bytes 14688256 | tf_op jit(solution)/shard_map/dot_general | solution.py:69
  235.0 3.7 convolution_convert_fusion.2
  238.7 85.3 %all-reduce.24.cloned.1.call-done = bf16[1024,1024]{1,0:T(8,128)(2,1)} async-done(((bf16[1024,1024]{1,0:T(8,128)(2,1)}), bf16[1024,1024]{1,0:T(8,128)(2,1)}) %all-reduce.24.cloned.1.call-update) | async-done | bytes 2097168 | tf_op jit(solution)/shard_map/psum | solution.py:75
  324.1 4.5 convert_reduce_fusion.1
  328.8 2.7 fusion.34
  331.5 2.4 fusion.72
  333.9 2.0 copy-done.3
  337.8 3.6 all-to-all-start.2
  341.5 8.8 %all-to-all-done.2 = bf16[2,512,256]{1,0,2:T(2,128)(2,1)S(1)} async-done(((bf16[2,512,256]{1,0,2:T(2,128)(2,1)}), bf16[2,512,256]{1,0,2:T(2,128)(2,1)S(1)}, u32[]{:S(2)}, u32[]{:S(2)}) %all-to-all-start.2) | async-done | bytes 524320 | tf_op jit(solution)/shard_map/all_to_all | solution.py:235
  351.6 103.6 %while.56 = (s32[]{:T(128)}, bf16[2,2048,64]{2,0,1:T(2,128)(2,1)}, bf16[2,2048,64]{1,2,0:T(8,128)(2,1)}, bf16[2,2048,64]{1,2,0:T(8,128)(2,1)}, bf16[2,2048,64]{2...) while((s32[]{:T(128)}, bf16[2,2048,64]{2,0,1:T(2,128)(2,1)}, ...), condition=%wide.region_19.20_spmd, body=%wide.region_15.19_spmd.sunk | while | flops 680164864 | bytes 41838996 | solution.py:241
  356.0 20.1 %while.58 = (s32[]{:T(128)}, f32[2048,64]{0,1:T(8,128)S(1)}, f32[2048,64]{0,1:T(8,128)S(1)}, f32[4,512,64]{1,2,0:T(8,128)}, bf16[4,512,64]{2,1,0:T(8,128)(2,1)S(...) while((s32[]{:T(128)}, f32[2048,64]{0,1:T(8,128)S(1)}, ...), condition=%wide.region_18.18_spmd.clone, body=%wide.region_16.17_spmd.clone.sunk | while | flops 680164864 | bytes 35530900 | solution.py:131
  374.6 1.5 fusion.133
  377.5 25.1 %dynamic_update_slice.47 = bf16[2,2048,64]{2,0,1:T(2,128)(2,1)} dynamic-update-slice(bf16[2,2048,64]{2,0,1:T(2,128)(2,1)} %get-tuple-element.800, f32[1,2048,64]{2,0,1:T(1,128)S(1)} %bitcast.276, s32[]{:T(128)S(6)} %copy.184, s32[]{:T(128)} %constant.81.clone.1..sunk.2, s32[]{:T(128)} %constant.81.clone.1..sunk.2) | dynamic-update-slice | bytes 1048580 | tf_op jit(solution)/shard_map/while/body/jit(dynamic_update_index_in_dim)/dynamic_update_slice | solution.py:241
  407.8 20.1 %while.58 = (s32[]{:T(128)}, f32[2048,64]{0,1:T(8,128)S(1)}, f32[2048,64]{0,1:T(8,128)S(1)}, f32[4,512,64]{1,2,0:T(8,128)}, bf16[4,512,64]{2,1,0:T(8,128)(2,1)S(...) while((s32[]{:T(128)}, f32[2048,64]{0,1:T(8,128)S(1)}, ...), condition=%wide.region_18.18_spmd.clone, body=%wide.region_16.17_spmd.clone.sunk | while | flops 680164864 | bytes 35530900 | solution.py:131
  426.4 1.5 fusion.133
  429.2 25.1 %dynamic_update_slice.47 = bf16[2,2048,64]{2,0,1:T(2,128)(2,1)} dynamic-update-slice(bf16[2,2048,64]{2,0,1:T(2,128)(2,1)} %get-tuple-element.800, f32[1,2048,64]{2,0,1:T(1,128)S(1)} %bitcast.276, s32[]{:T(128)S(6)} %copy.184, s32[]{:T(128)} %constant.81.clone.1..sunk.2, s32[]{:T(128)} %constant.81.clone.1..sunk.2) | dynamic-update-slice | bytes 1048580 | tf_op jit(solution)/shard_map/while/body/jit(dynamic_update_index_in_dim)/dynamic_update_slice | solution.py:241
  455.2 3.6 copy.137
  458.8 3.6 copy.136
  462.3 7.2 fusion.81
  469.5 3.3 reshape.258
  472.8 4.3 all-to-all-start.3
  478.0 4.7 multiply_convert_fusion.1
  484.1 3.7 convolution_convert_fusion.3
  487.7 9.6 %all-to-all-done.3 = bf16[4,2,98304]{2,1,0:T(2,128)(2,1)} async-done(((bf16[4,2,98304]{2,1,0:T(2,128)(2,1)}), bf16[4,2,98304]{2,1,0:T(2,128)(2,1)}, u32[]{:S(2)}, u32[]{:S(2)}) %all-to-all-start.3) | async-done | bytes 1572896 | tf_op jit(solution)/shard_map/all_to_all | solution.py:251
  497.3 3.8 reshape.259
  501.0 6.4 copy.88
  507.5 1.5 slice.204
  515.8 4.7 bitcast_convert_fusion
  521.6 3.7 convolution_convert_fusion.5
  525.6 5.4 convolution_convert_fusion
  531.2 6.9 convolution_convert_fusion.1
  538.2 135.6 %all-reduce.26.cloned.1.call-done = (bf16[1024,1024]{1,0:T(8,128)(2,1)}, bf16[1024,1024]{1,0:T(8,128)(2,1)}) async-done(((bf16[1024,1024]{1,0:T(8,128)(2,1)}, bf16[1024,1024]{1,0:T(8,128)(2,1)}), (bf16[1024,1024]{1,0:T(8,128)(2,1)}, bf16[1024,1024]{1,0:T(8,128)(2,1)})) %all-reduce.26.cloned.1.call-update) | async-done | bytes 4194320 | tf_op jit(solution)/shard_map/psum | solution.py:75
  673.9 3.1 convert_reduce_fusion
  677.0 3.1 fusion.35
  680.1 3.0 fusion.61
  683.3 25.0 %reduce-scatter.5.cloned.1.call-done = bf16[3,512,256]{1,2,0:T(8,128)(2,1)} async-done(((bf16[3,1024,256]{1,2,0:T(8,128)(2,1)}), bf16[3,512,256]{1,2,0:T(8,128)(2,1)}) %reduce-scatter.5.cloned.1.call-update) | async-done | bytes 786448 | tf_op jit(solution)/shard_map/reduce_scatter | solution.py:287
  708.4 2.0 convert_reduce_fusion.3
  711.7 25.7 %all-reduce.14 = (f32[3,256]{1,0:T(4,128)}, f32[1024]{0:T(1024)}, f32[2,1024]{1,0:T(2,128)}, f32[2,1024]{1,0:T(2,128)}, f32[2,1024]{1,0:T(2,128)}) all-reduce(f32[3,256]{1,0:T(4,128)S(1)} %convert_reduce_fusion.5, f32[1024]{0:T(1024)S(1)} %copy-done.61, ...), channel_id=1, replica_groups=mesh['fsdp'=2,'ctx'=4,'tp'=4] {'fsdp','ctx'}, use_global_device_ids=true, to_apply=%region_26.27 | all-reduce | flops 7936 | bytes 63488 | tf_op jit(solution)/shard_map/psum | solution.py:306
  737.4 7.1 add_add_fusion.2
  744.6 33.1 %all-reduce.28.cloned.1.call-done = (bf16[3,512,256]{1,2,0:T(8,128)(2,1)}, bf16[256,512]{1,0:T(8,128)(2,1)}, bf16[512,1024]{1,0:T(8,128)(2,1)}, bf16[1024,512]{1,0:T(8,128)(2,1)}) async-done(((bf16[3,512,256]{1,2,0:T(8,128)(2,1)}, bf16[256,512]{1,0:T(8,128)(2,1)}, bf16[512,1024]{1,0:T(8,128)(2,1)}, bf16[1024,512]{1,0:T(8,128)(2,1)}), (bf16[3,512,256]{1,2,0:T(8,128)(2,1)}, bf16[256,512]{1,0:T(8,128)(2,1)}, ...) | async-done | bytes 3145744 | tf_op jit(solution)/shard_map/psum | solution.py:301
  777.6 1.9 convert_element_type.176
  779.5 2.5 copy.93
  782.1 2.8 convert_element_type.178
  784.9 1.6 convert_element_type.181
  (356 shorter events, 111.8 us)
Async XLA Ops:
  8.0 10.6 %copy-start = (bf16[2,512,1024]{2,1,0:T(8,128)(2,1)S(1)}, bf16[2,512,1024]{2,1,0:T(8,128)(2,1)}, u32[]{:S(2)}) copy-start(bf16[2,512,1024]{2,1,0:T(8,128)(2,1)} %param.20) | copy-start | bytes 6291460
  8.0 7.9 copy-start.54
  8.0 8.5 %copy-start.55 = (f32[2,1024]{1,0:T(2,128)S(1)}, f32[2,1024]{1,0:T(2,128)}, u32[]{:S(2)}) copy-start(f32[2,1024]{1,0:T(2,128)} %param.29) | copy-start | bytes 24580
  8.0 9.1 %copy-start.53 = (s32[3,2,512]{2,1,0:T(2,128)S(1)}, s32[3,2,512]{2,1,0:T(2,128)}, u32[]{:S(2)}) copy-start(s32[3,2,512]{2,1,0:T(2,128)} %param.21) | copy-start | bytes 36868
  8.1 20.8 %collective-permute-start = (bf16[1,3,512,256]{3,2,1,0:T(8,128)(2,1)}, bf16[1,3,512,256]{3,2,1,0:T(8,128)(2,1)S(1)}, u32[]{:S(2)}, u32[]{:S(2)}) collective-permute-start(bf16[1,3,512,256]{3,2,1,0:T(8,128)(2,1)} %bitcast.298), channel_id=1, source_target_pairs={{0,16},{16,0},{1,17},{17,1},{2,18},{18,2},{3,19},{19,3},{4,20},{20... | collective-permute-start | bytes 2359304 | tf_op jit(solution)/shard_map/ppermute | solution.py:27
  13.1 15.8 %copy-start.14 = (bf16[3,512,256]{2,1,0:T(8,128)(2,1)S(1)}, bf16[3,512,256]{2,1,0:T(8,128)(2,1)}, u32[]{:S(2)}) copy-start(bf16[3,512,256]{2,1,0:T(8,128)(2,1)} %param.22) | copy-start | bytes 2359300
  16.6 12.5 %copy-start.37 = (f32[1,1024]{1,0:T(1,128)}, f32[1,1024]{1,0:T(1,128)S(1)}, u32[]{:S(2)}) copy-start(f32[1,1024]{1,0:T(1,128)S(1)} %get-tuple-element.445) | copy-start | bytes 12292
  17.2 11.9 %copy-start.45 = (f32[1,1024]{1,0:T(1,128)}, f32[1,1024]{1,0:T(1,128)S(1)}, u32[]{:S(2)}) copy-start(f32[1,1024]{1,0:T(1,128)S(1)} %get-tuple-element.447) | copy-start | bytes 12292
  18.6 13.4 %copy-start.21 = (f32[1024,10]{0,1:T(8,128)}, f32[1024,10]{0,1:T(8,128)S(1)}, u32[]{:S(2)}) copy-start(f32[1024,10]{0,1:T(8,128)S(1)} %get-tuple-element.437) | copy-start | bytes 122884
  18.6 13.4 %copy-start.23 = (f32[1024,10]{0,1:T(8,128)}, f32[1024,10]{0,1:T(8,128)S(1)}, u32[]{:S(2)}) copy-start(f32[1024,10]{0,1:T(8,128)S(1)} %get-tuple-element.438) | copy-start | bytes 122884
  18.6 13.4 %copy-start.25 = (f32[1024,10]{0,1:T(8,128)}, f32[1024,10]{0,1:T(8,128)S(1)}, u32[]{:S(2)}) copy-start(f32[1024,10]{0,1:T(8,128)S(1)} %get-tuple-element.439) | copy-start | bytes 122884
  18.6 13.4 %copy-start.27 = (f32[1024,10]{0,1:T(8,128)}, f32[1024,10]{0,1:T(8,128)S(1)}, u32[]{:S(2)}) copy-start(f32[1024,10]{0,1:T(8,128)S(1)} %get-tuple-element.454) | copy-start | bytes 122884
  18.6 13.4 %copy-start.29 = (f32[1024,10]{0,1:T(8,128)}, f32[1024,10]{0,1:T(8,128)S(1)}, u32[]{:S(2)}) copy-start(f32[1024,10]{0,1:T(8,128)S(1)} %get-tuple-element.455) | copy-start | bytes 122884
  18.6 13.4 %copy-start.31 = (f32[1024,10]{0,1:T(8,128)}, f32[1024,10]{0,1:T(8,128)S(1)}, u32[]{:S(2)}) copy-start(f32[1024,10]{0,1:T(8,128)S(1)} %get-tuple-element.456) | copy-start | bytes 122884
  19.5 9.9 %copy-start.64 = (f32[3,256]{1,0:T(4,128)S(1)}, f32[3,256]{1,0:T(4,128)}, u32[]{:S(2)}) copy-start(f32[3,256]{1,0:T(4,128)} %param.23) | copy-start | bytes 9220
  39.2 23.8 %all-to-all-start = ((bf16[3,2,512,256]{2,1,0,3:T(2,128)(2,1)}), bf16[3,2,512,256]{2,1,0,3:T(2,128)(2,1)S(1)}, u32[]{:S(2)}, u32[]{:S(2)}) async-start(bf16[3,2,512,256]{2,1,0,3:T(2,128)(2,1)} %pad_maximum_fusion.2), calls=%async_computation | async-start | bytes 3145728 | tf_op jit(solution)/shard_map/all_to_all | solution.py:185
  69.0 11.4 %copy-start.34 = (bf16[2,4,512,64]{2,3,1,0:T(8,128)(2,1)S(1)}, bf16[2,4,512,64]{2,3,1,0:T(8,128)(2,1)}, u32[]{:S(2)}) copy-start(bf16[2,4,512,64]{2,3,1,0:T(8,128)(2,1)} %get-tuple-element.767) | copy-start | bytes 1572868 | tf_op jit(solution)/shard_map/while
  82.6 11.4 %copy-start.34 = (bf16[2,4,512,64]{2,3,1,0:T(8,128)(2,1)S(1)}, bf16[2,4,512,64]{2,3,1,0:T(8,128)(2,1)}, u32[]{:S(2)}) copy-start(bf16[2,4,512,64]{2,3,1,0:T(8,128)(2,1)} %get-tuple-element.767) | copy-start | bytes 1572868 | tf_op jit(solution)/shard_map/while
  94.8 18.6 %copy-start.5 = (bf16[2,2048,64]{2,1,0:T(8,128)(2,1)}, bf16[2,2048,64]{2,1,0:T(8,128)(2,1)S(1)}, u32[]{:S(2)}) copy-start(bf16[2,2048,64]{2,1,0:T(8,128)(2,1)S(1)} %get-tuple-element.846) | copy-start | bytes 1572868
  94.8 7.7 copy-start.36
  99.0 12.8 %all-to-all-start.1 = ((bf16[4,2,32768]{2,1,0:T(2,128)(2,1)}), bf16[4,2,32768]{2,1,0:T(2,128)(2,1)S(1)}, u32[]{:S(2)}, u32[]{:S(2)}) async-start(bf16[4,2,32768]{2,1,0:T(2,128)(2,1)} %reshape.256), calls=%async_computation.1 | async-start | bytes 1048576 | tf_op jit(solution)/shard_map/all_to_all | solution.py:198
  102.5 101.8 %all-reduce.22.cloned.1.call-start = ((), (), s32[]{:S(2)}) async-start(), calls=%async_computation.8 | async-start | bytes 4194304 | tf_op jit(solution)/shard_map/psum | solution.py:75
  113.4 4.2 copy-start.56
  113.4 90.9 %copy-start.1 = (bf16[2,512,1024]{2,1,0:T(8,128)(2,1)S(1)}, bf16[2,512,1024]{2,1,0:T(8,128)(2,1)}, u32[]{:S(2)}) copy-start(bf16[2,512,1024]{2,1,0:T(8,128)(2,1)} %param.20) | copy-start | bytes 6291460
  116.4 93.5 %all-gather.4.cloned.1.call-start = ((), (), s32[]{:S(2)}) async-start(), calls=%async_computation.9 | async-start | bytes 3145728 | tf_op jit(solution)/shard_map/all_gather | solution.py:163
  117.0 100.3 %all-gather.6.cloned.1.call-start = ((), (), s32[]{:S(2)}) async-start(), calls=%async_computation.10 | async-start | bytes 3145728 | tf_op jit(solution)/shard_map/all_gather | solution.py:164
  117.5 206.5 %all-reduce.24.cloned.1.call-start = ((), (), s32[]{:S(2)}) async-start(), calls=%async_computation.11 | async-start | bytes 4194304 | tf_op jit(solution)/shard_map/psum | solution.py:75
  118.2 91.6 %copy-start.41 = (f32[1,1024]{1,0:T(1,128)}, f32[1,1024]{1,0:T(1,128)S(1)}, u32[]{:S(2)}) copy-start(f32[1,1024]{1,0:T(1,128)S(1)} %get-tuple-element.443) | copy-start | bytes 12292
  209.8 121.7 %copy-start.43 = (f32[1024]{0:T(1024)}, f32[1024]{0:T(1024)S(1)}, u32[]{:S(2)}) copy-start(f32[1024]{0:T(1024)S(1)} %fusion.66) | copy-start | bytes 12292
  209.9 7.4 copy-start.10
  209.9 7.4 copy-start.57
  217.3 17.7 %copy-start.63 = (bf16[1024,1024]{1,0:T(8,128)(2,1)S(1)}, bf16[1024,1024]{1,0:T(8,128)(2,1)}, u32[]{:S(2)}) copy-start(bf16[1024,1024]{1,0:T(8,128)(2,1)} %all-gather.4.cloned.1.call-done) | copy-start | bytes 6291460
  324.1 4.5 copy-start.4
  324.1 4.7 copy-start.7
  337.8 12.4 %all-to-all-start.2 = ((bf16[2,512,256]{1,0,2:T(2,128)(2,1)}), bf16[2,512,256]{1,0,2:T(2,128)(2,1)S(1)}, u32[]{:S(2)}, u32[]{:S(2)}) async-start(bf16[2,512,256]{1,0,2:T(2,128)(2,1)} %copy.79), calls=%async_computation.2 | async-start | bytes 1048576 | tf_op jit(solution)/shard_map/all_to_all | solution.py:235
  469.5 8.5 %copy-start.58 = (f32[1024]{0:T(1024)S(1)}, f32[1024]{0:T(1024)}, u32[]{:S(2)}) copy-start(f32[1024]{0:T(1024)} %param.26) | copy-start | bytes 12292
  472.8 24.5 %all-to-all-start.3 = ((bf16[4,2,98304]{2,1,0:T(2,128)(2,1)}), bf16[4,2,98304]{2,1,0:T(2,128)(2,1)}, u32[]{:S(2)}, u32[]{:S(2)}) async-start(bf16[4,2,98304]{2,1,0:T(2,128)(2,1)} %reshape.258), calls=%async_computation.3 | async-start | bytes 3145728 | tf_op jit(solution)/shard_map/all_to_all | solution.py:251
  477.2 38.7 %all-gather.8.cloned.1.call-start = ((), (), s32[]{:S(2)}) async-start(), calls=%async_computation.12 | async-start | bytes 2359296 | tf_op jit(solution)/shard_map/all_gather | solution.py:210
  477.7 196.1 %all-reduce.26.cloned.1.call-start = ((), (), s32[]{:S(2)}) async-start(), calls=%async_computation.17 | async-start | bytes 8388608 | tf_op jit(solution)/shard_map/psum | solution.py:75
  478.0 6.0 copy-start.62
  515.8 4.8 copy-start.19
  520.5 5.1 copy-start.11
  520.6 162.7 %reduce-scatter.7.cloned.1.call-start = ((), (), s32[]{:S(2)}) async-start(), calls=%async_computation.14 | async-start | bytes 786432 | tf_op jit(solution)/shard_map/reduce_scatter | solution.py:290
  525.3 5.9 copy-start.40
  525.3 5.9 copy-start.44
  525.3 5.9 copy-start.60
  525.3 157.9 %reduce-scatter.11.cloned.1.call-start = ((), (), s32[]{:S(2)}) async-start(), calls=%async_computation.16 | async-start | bytes 3145728 | tf_op jit(solution)/shard_map/reduce_scatter | solution.py:296
  531.1 7.1 copy-start.48
  531.1 7.1 copy-start.49
  531.1 142.8 %copy-start.2 = (bf16[2,512,1024]{2,1,0:T(8,128)(2,1)S(1)}, bf16[2,512,1024]{2,1,0:T(8,128)(2,1)}, u32[]{:S(2)}) copy-start(bf16[2,512,1024]{2,1,0:T(8,128)(2,1)} %param.20) | copy-start | bytes 6291460
  531.1 142.8 %copy-start.38 = (f32[1,1024]{1,0:T(1,128)S(1)}, f32[1,1024]{1,0:T(1,128)}, u32[]{:S(2)}) copy-start(f32[1,1024]{1,0:T(1,128)} %copy-done.37) | copy-start | bytes 12292
  531.1 152.2 %reduce-scatter.9.cloned.1.call-start = ((), (), s32[]{:S(2)}) async-start(), calls=%async_computation.15 | async-start | bytes 3145728 | tf_op jit(solution)/shard_map/reduce_scatter | solution.py:293
  538.1 138.9 %copy-start.46 = (f32[1,1024]{1,0:T(1,128)S(1)}, f32[1,1024]{1,0:T(1,128)}, u32[]{:S(2)}) copy-start(f32[1,1024]{1,0:T(1,128)} %copy-done.45) | copy-start | bytes 12292
  538.1 170.2 %reduce-scatter.5.cloned.1.call-start = ((), (), s32[]{:S(2)}) async-start(), calls=%async_computation.13 | async-start | bytes 2359296 | tf_op jit(solution)/shard_map/reduce_scatter | solution.py:287
  676.9 3.2 copy-start.18
  677.0 3.2 copy-start.20
  683.1 27.2 %copy-start.47 = (f32[1024]{0:T(1024)S(1)}, f32[1024]{0:T(1024)}, u32[]{:S(2)}) copy-start(f32[1024]{0:T(1024)} %get-tuple-element.369) | copy-start | bytes 12292
  683.1 28.5 %copy-start.50 = (f32[1024]{0:T(1024)S(1)}, f32[1024]{0:T(1024)}, u32[]{:S(2)}) copy-start(f32[1024]{0:T(1024)} %get-tuple-element.296) | copy-start | bytes 12292
  683.1 28.6 %copy-start.51 = (f32[1024]{0:T(1024)S(1)}, f32[1024]{0:T(1024)}, u32[]{:S(2)}) copy-start(f32[1024]{0:T(1024)} %get-tuple-element.290) | copy-start | bytes 12292
  683.1 28.6 %copy-start.61 = (f32[1024]{0:T(1024)S(1)}, f32[1024]{0:T(1024)}, u32[]{:S(2)}) copy-start(f32[1024]{0:T(1024)} %get-tuple-element.371) | copy-start | bytes 12292
  683.1 54.3 %copy-start.42 = (f32[1,1024]{1,0:T(1,128)S(1)}, f32[1,1024]{1,0:T(1,128)}, u32[]{:S(2)}) copy-start(f32[1,1024]{1,0:T(1,128)} %copy-done.41) | copy-start | bytes 12292
  683.1 54.3 %copy-start.52 = (f32[1,1024]{1,0:T(1,128)S(1)}, f32[1,1024]{1,0:T(1,128)}, u32[]{:S(2)}) copy-start(f32[1,1024]{1,0:T(1,128)} %get-tuple-element.442) | copy-start | bytes 12292
  683.2 94.4 %all-reduce.28.cloned.1.call-start = ((), (), s32[]{:S(2)}) async-start(), calls=%async_computation.18 | async-start | bytes 6291456 | tf_op jit(solution)/shard_map/psum | solution.py:301
  777.6 7.2 copy-start.33
  (20 other events, 36.5 us)
Sparse Core Ops, SparseCore 0:
  116.5 87.7 all-reduce.21
  238.9 85.1 all-reduce.23
  520.7 153.1 all-reduce.25
  708.5 69.0 all-reduce.27
Sparse Core Ops, SparseCore 1:
  118.4 34.5 all-gather.3
  154.4 32.9 all-gather.5
  479.2 26.5 all-gather.7
  525.4 12.7 reduce-scatter.6
  540.4 31.8 reduce-scatter.10
  574.5 31.8 reduce-scatter.8
  683.3 25.0 reduce-scatter.4
